TPU v7x, 32 devices: a whole 2x2x4 slice. The times are simulated.
32 devices in a mesh: head: 8 (over z, core), kv: 4 (over y, x).
Axes of the slice: x: 2, y: 2, z: 4, core: 2. Of those that a mesh axis runs over, the one named last changes fastest.
Arguments:
- queries: bfloat16 [2048, 8192], P(('kv', 'head')), may hold values from -6 to 6
- key_rows: bfloat16 [2048, 1024], P(('kv', 'head')), may hold values from -6 to 6
- value_matrix: bfloat16 [2048, 1024], P(('kv', 'head')), may hold values from -6 to 6
- doc_ids: int32 [2048], P(('kv', 'head')), may hold values from 0 to 5, as said below
Outputs:
- attended: bfloat16 [2048, 8192], P(('kv', 'head'))
Inputs may be any that keep to these rules, and one draw needn't show every extreme that they name: doc_ids starts at 0, never falls, and rises by one at the first token of each of the 6 documents; every document starts at an even position and has 2 tokens or more.
All inputs are finite; a program needn't handle non-finite values.
Results may differ from a plain program's by a relative error of at most 0.015.
Values may be sent and summed in bfloat16 or wider, within the bound.
A program may use at most 64 MiB of HBM per device.

v0:
```python
import math
import jax
import jax.numpy as jnp
from jax import lax
from jax.sharding import PartitionSpec as P

QUERY_HEADS = 64
KEY_VALUE_HEADS = 8
HEAD_SIZE = 128
NEG_FILL = -1e30


def repeat_heads(input_matrix, head_repeats):
    row_number = input_matrix.shape[0]
    heads_apart = input_matrix.reshape(row_number, KEY_VALUE_HEADS, 1, HEAD_SIZE)
    expanded_heads = jnp.broadcast_to(
        heads_apart, (row_number, KEY_VALUE_HEADS, head_repeats, HEAD_SIZE)
    )
    return expanded_heads.reshape(row_number, KEY_VALUE_HEADS * head_repeats * HEAD_SIZE)


def block_terms(query_group, query_pos, query_doc, key_block, value_block, key_pos, key_doc):
    key_count = key_block.shape[0]
    key_value_slot = query_group.shape[1]
    key_heads = key_block.reshape(key_count, key_value_slot, HEAD_SIZE)
    value_heads = value_block.reshape(key_count, key_value_slot, HEAD_SIZE)
    scores = jnp.einsum(
        "rkgd,ckd->kgrc", query_group, key_heads, preferred_element_type=jnp.float32
    ) * HEAD_SIZE ** (-0.5)
    allowed = (key_pos[None, :] <= query_pos[:, None]) & (key_doc[None, :] == query_doc[:, None])
    masked = jnp.where(allowed, scores, NEG_FILL)
    row_peak = jnp.max(masked, axis=-1)
    weights = jnp.where(allowed, jnp.exp(masked - row_peak[..., None]), 0.0)
    row_total = jnp.sum(weights, axis=-1)
    weighted = jnp.einsum(
        "kgrc,ckd->kgrd",
        weights.astype(jnp.bfloat16),
        value_heads,
        preferred_element_type=jnp.float32,
    )
    return (row_peak, row_total, weighted)


def attend_block(query_group, query_pos, query_doc, key_block, value_block, key_pos, key_doc):
    return block_terms(query_group, query_pos, query_doc, key_block, value_block, key_pos, key_doc)


def combine_terms(first_terms, second_terms):
    joint_peak = jnp.maximum(first_terms[0], second_terms[0])
    left_factor = jnp.exp(first_terms[0] - joint_peak)
    right_factor = jnp.exp(second_terms[0] - joint_peak)
    joint_total = first_terms[1] * left_factor + second_terms[1] * right_factor
    joint_weighted = (
        first_terms[2] * left_factor[..., None] + second_terms[2] * right_factor[..., None]
    )
    return (joint_peak, joint_total, joint_weighted)


def local(queries, key_rows, value_matrix, doc_ids):
    head_number = lax.axis_size("head")
    head_repeats = max(1, head_number // KEY_VALUE_HEADS)
    key_send = repeat_heads(key_rows, head_repeats)
    value_send = repeat_heads(value_matrix, head_repeats)
    query_block, key_block, value_block = (
        lax.all_to_all(queries, "head", split_axis=1, concat_axis=0, tiled=True),
        lax.all_to_all(key_send, "head", split_axis=1, concat_axis=0, tiled=True),
        lax.all_to_all(value_send, "head", split_axis=1, concat_axis=0, tiled=True),
    )
    block_len = query_block.shape[0]
    doc_global = lax.all_gather(doc_ids, ("kv", "head"), axis=0, tiled=True)
    query_width = query_block.shape[1]
    present_heads = query_width // HEAD_SIZE
    key_value_slot = max(1, present_heads // (QUERY_HEADS // KEY_VALUE_HEADS))
    group_here = present_heads // key_value_slot
    own_first = lax.axis_index("kv") * block_len
    own_pos = own_first + jnp.arange(block_len, dtype=jnp.int32)
    own_doc = jnp.take(doc_global, own_pos)
    query_group = query_block.reshape(block_len, key_value_slot, group_here, HEAD_SIZE)
    term_shape = (key_value_slot, group_here, block_len)
    initial = (
        jnp.full(term_shape, NEG_FILL, jnp.float32),
        jnp.zeros(term_shape, jnp.float32),
        jnp.zeros(term_shape + (HEAD_SIZE,), jnp.float32),
    )
    key_piece = lax.all_gather(key_block, "kv", axis=0, tiled=True)
    value_piece = lax.all_gather(value_block, "kv", axis=0, tiled=True)
    piece_rows = key_piece.shape[0]
    step_rows = math.gcd(piece_rows, 1024)

    def one_step(step_index, inner):
        local_first = step_index * step_rows
        keys_now = lax.dynamic_slice_in_dim(key_piece, local_first, step_rows, 0)
        values_now = lax.dynamic_slice_in_dim(value_piece, local_first, step_rows, 0)
        key_pos = local_first + jnp.arange(step_rows, dtype=jnp.int32)
        key_doc = jnp.take(doc_global, key_pos)
        return combine_terms(
            inner,
            attend_block(query_group, own_pos, own_doc, keys_now, values_now, key_pos, key_doc),
        )

    folded = lax.fori_loop(0, piece_rows // step_rows, one_step, initial)
    result = (
        (folded[2] / folded[1][..., None]).transpose(2, 0, 1, 3).reshape(block_len, query_width)
    )
    result = result.astype(jnp.bfloat16)
    return lax.all_to_all(result, "head", split_axis=0, concat_axis=1, tiled=True)


def solution(mesh):
    return jax.shard_map(
        local,
        mesh=mesh,
        in_specs=(
            P(("kv", "head"), None),
            P(("kv", "head"), None),
            P(("kv", "head"), None),
            P(("kv", "head")),
        ),
        out_specs=P(("kv", "head"), None),
        check_vma=False,
    )
```

profile of v0, /device:TPU:0, one launch (start us, length us, event | category | flops | bytes accessed | tf_op | source)
XLA Modules:
  0.0 176.7 jit_solution(10033229204570758715)
XLA Ops:
  0.0 0.0 copy-start
  0.0 0.9 copy-done
  0.9 0.7 copy_bitcast_fusion.2
  1.6 6.4 %all-to-all-start = ((bf16[64,8,128]{2,0,1:T(8,128)(2,1)}), bf16[64,8,128]{2,0,1:T(8,128)(2,1)S(1)}, u32[]{:S(2)}, u32[]{:S(2)}) async-start(bf16[64,8,128]{2,0,1:T(8,128)(2,1)} %copy_bitcast_fusion.2), calls=%async_computation | async-start | bytes 262144 | tf_op jit(solution)/shard_map/all_to_all | solution.py:66
  7.9 1.6 copy_bitcast_fusion.1
  9.5 5.2 %all-to-all-done = bf16[64,8,128]{2,0,1:T(8,128)(2,1)S(1)} async-done(((bf16[64,8,128]{2,0,1:T(8,128)(2,1)}), bf16[64,8,128]{2,0,1:T(8,128)(2,1)S(1)}, u32[]{:S(2)}, u32[]{:S(2)}) %all-to-all-start) | async-done | bytes 131104 | tf_op jit(solution)/shard_map/all_to_all | solution.py:66
  14.7 3.4 %all-to-all-start.2 = ((bf16[64,8,128]{2,0,1:T(8,128)(2,1)}), bf16[64,8,128]{2,0,1:T(8,128)(2,1)S(1)}, u32[]{:S(2)}, u32[]{:S(2)}) async-start(bf16[64,8,128]{2,0,1:T(8,128)(2,1)} %copy_bitcast_fusion.1), calls=%async_computation.2 | async-start | bytes 262144 | tf_op jit(solution)/shard_map/all_to_all | solution.py:67
  18.1 2.3 %copy.30 = bf16[8,8,8,1024]{3,2,0,1:T(8,128)(2,1)} copy(bf16[8,8,8,1024]{3,2,1,0:T(8,128)(2,1)} %bitcast.121) | data formatting | bytes 2097152 | tf_op jit(solution)/shard_map/all_to_all | solution.py:65
  20.4 4.4 %all-to-all-done.2 = bf16[64,8,128]{2,0,1:T(8,128)(2,1)S(1)} async-done(((bf16[64,8,128]{2,0,1:T(8,128)(2,1)}), bf16[64,8,128]{2,0,1:T(8,128)(2,1)S(1)}, u32[]{:S(2)}, u32[]{:S(2)}) %all-to-all-start.2) | async-done | bytes 131104 | tf_op jit(solution)/shard_map/all_to_all | solution.py:67
  24.8 3.6 %all-to-all-start.1 = ((bf16[64,8,1024]{2,0,1:T(8,128)(2,1)}), bf16[64,8,1024]{2,0,1:T(8,128)(2,1)S(1)}, u32[]{:S(2)}, u32[]{:S(2)}) async-start(bf16[64,8,1024]{2,0,1:T(8,128)(2,1)} %bitcast.93), calls=%async_computation.1 | async-start | bytes 2097152 | tf_op jit(solution)/shard_map/all_to_all | solution.py:65
  28.4 1.3 dynamic-slice
  30.4 0.9 dynamic-update-slice
  31.2 43.9 %all-reduce = s32[2048]{0:T(1024)S(1)} all-reduce(s32[2048]{0:T(1024)S(1)} %dynamic-update-slice), channel_id=1, replica_groups=mesh['head'=8,'kv'=4] {'kv','head'}, use_global_device_ids=true, to_apply=%add | all-reduce | flops 2048 | bytes 16384
  75.2 3.1 %gather_fusion.1 = s32[512]{0:T(512)S(1)} fusion(s32[2048]{0:T(1024)S(1)} %all-reduce, s32[1024]{0:T(1024)S(1)} %pad_clamp_fusion), kind=kCustom, calls=%fused_computation.1 | custom fusion | bytes 6144 | tf_op jit(solution)/shard_map/jit(_take)/gather | solution.py:77
  78.3 11.6 %all_gather.11 = bf16[2048,128]{1,0:T(8,128)(2,1)S(1)} all-gather(bf16[512,128]{1,0:T(8,128)(2,1)S(1)} %bitcast.124), channel_id=1, replica_groups=mesh['head'=8,'kv'=4] {'kv'}, dimensions={0}, use_global_device_ids=true | all-gather | bytes 655360 | tf_op jit(solution)/shard_map/all_gather | solution.py:86
  89.9 9.0 %all_gather.10 = bf16[2048,128]{1,0:T(8,128)(2,1)S(1)} all-gather(bf16[512,128]{1,0:T(8,128)(2,1)S(1)} %bitcast.123), channel_id=1, replica_groups=mesh['head'=8,'kv'=4] {'kv'}, dimensions={0}, use_global_device_ids=true | all-gather | bytes 655360 | tf_op jit(solution)/shard_map/all_gather | solution.py:85
  98.9 0.0 all-to-all-done.1
  98.9 0.3 copy.26
  99.2 0.1 copy.18
  99.3 43.2 %while.18 = (s32[]{:T(128)}, f32[1,8,512]{2,1,0:T(8,128)S(1)}, f32[1,8,512]{2,1,0:T(8,128)S(1)}, f32[1,8,512,128]{3,2,1,0:T(8,128)}, s32[2048]{0:T(1024)S(1)}, /...) while((s32[]{:T(128)}, f32[1,8,512]{2,1,0:T(8,128)S(1)}, ...), condition=%wide.region_3.4_spmd.clone, body=%wide.region_0.3_spmd.clone.sunk | while | flops 2205726208 | bytes 75335952 | solution.py:101
  99.4 6.2 %gather_fusion = s32[1024]{0:T(1024)S(1)} fusion(s32[2048]{0:T(1024)S(1)} %get-tuple-element.370, s32[1024]{0:T(1024)S(1)} %broadcast_clamp_fusion.2), kind=kCustom, calls=%fused_computation.clone.clone.1 | custom fusion | bytes 12288 | tf_op jit(solution)/shard_map/while/body/eval_jaxpr/jit(_take)/gather | solution.py:95
  105.6 0.8 compare_and_fusion.2
  106.4 2.9 %fusion.41 = (f32[8,512]{1,0:T(8,128)S(1)}, f32[1024,512,8]{1,0,2:T(8,128)S(1)}) fusion(pred[512,1024]{0,1:T(8,128)(4,1)S(1)} %compare_and_fusion.2, bf16[512,1,8,128]{3,0,2,1:T(8,128)(2,1)S(1)} %get-tuple-element.373, bf16[2048,128]{1,0:T(8,128)(2,1)S(1)} %get-tuple-element.372, s32[]{:T(128)S(6)} %select_n.145), kind=kOutput, calls=%fused_computation.5.clone.1 | convolution fusion | flops 1086320640 | bytes 18628612 | tf_op jit(solution)/shard_map/while/body/eval_jaxpr/rkgd,ckd->kgrc/dot_general | solution.py:27
  109.3 0.0 copy-start.1
  109.3 4.0 %fusion.43 = f32[8,512]{1,0:T(8,128)S(1)} fusion(f32[1024,512,8]{1,0,2:T(8,128)S(1)} %get-tuple-element.334, f32[8,512]{1,0:T(8,128)S(1)} %get-tuple-element.332, pred[512,1024]{0,1:T(8,128)(4,1)S(1)} %compare_and_fusion.2), kind=kLoop, calls=%fused_computation.7.clone.1 | loop fusion | flops 20967424 | bytes 17334272 | tf_op jit(solution)/shard_map/while/body/eval_jaxpr/reduce_sum | solution.py:34
  113.4 0.0 copy-done.1
  113.4 6.1 %bitcast_add_fusion.2 = f32[1,8,512,128]{3,2,1,0:T(8,128)S(1)} fusion(f32[1,8,512,128]{3,2,1,0:T(8,128)S(1)} %copy-done.1, f32[1024,512,8]{1,0,2:T(8,128)S(1)} %get-tuple-element.334, f32[8,512]{1,0:T(8,128)S(1)} %get-tuple-element.332, pred[512,1024]{0,1:T(8,128)(4,1)S(1)} %compare_and_fusion.2, f32[8,512]{1,0:T(8,128)S(1)} %get-tuple-element.336, ...), kind=kOutput, calls=%fused_computation.11.clone.1 | convolution fusion | flops 1096810496 | bytes 21807108 | tf_op jit(solution)/shard_map/while/body/eval_jaxpr/kgrc,ckd->kgrd/dot_general | solution.py:35
  119.6 0.0 copy-start.2
  119.6 1.3 copy-done.2
  120.9 6.2 %gather_fusion = s32[1024]{0:T(1024)S(1)} fusion(s32[2048]{0:T(1024)S(1)} %get-tuple-element.370, s32[1024]{0:T(1024)S(1)} %broadcast_clamp_fusion.2), kind=kCustom, calls=%fused_computation.clone.clone.1 | custom fusion | bytes 12288 | tf_op jit(solution)/shard_map/while/body/eval_jaxpr/jit(_take)/gather | solution.py:95
  127.1 0.8 compare_and_fusion.2
  128.0 2.9 %fusion.41 = (f32[8,512]{1,0:T(8,128)S(1)}, f32[1024,512,8]{1,0,2:T(8,128)S(1)}) fusion(pred[512,1024]{0,1:T(8,128)(4,1)S(1)} %compare_and_fusion.2, bf16[512,1,8,128]{3,0,2,1:T(8,128)(2,1)S(1)} %get-tuple-element.373, bf16[2048,128]{1,0:T(8,128)(2,1)S(1)} %get-tuple-element.372, s32[]{:T(128)S(6)} %select_n.145), kind=kOutput, calls=%fused_computation.5.clone.1 | convolution fusion | flops 1086320640 | bytes 18628612 | tf_op jit(solution)/shard_map/while/body/eval_jaxpr/rkgd,ckd->kgrc/dot_general | solution.py:27
  130.9 0.0 copy-start.1
  130.9 4.0 %fusion.43 = f32[8,512]{1,0:T(8,128)S(1)} fusion(f32[1024,512,8]{1,0,2:T(8,128)S(1)} %get-tuple-element.334, f32[8,512]{1,0:T(8,128)S(1)} %get-tuple-element.332, pred[512,1024]{0,1:T(8,128)(4,1)S(1)} %compare_and_fusion.2), kind=kLoop, calls=%fused_computation.7.clone.1 | loop fusion | flops 20967424 | bytes 17334272 | tf_op jit(solution)/shard_map/while/body/eval_jaxpr/reduce_sum | solution.py:34
  135.0 0.0 copy-done.1
  135.0 6.1 %bitcast_add_fusion.2 = f32[1,8,512,128]{3,2,1,0:T(8,128)S(1)} fusion(f32[1,8,512,128]{3,2,1,0:T(8,128)S(1)} %copy-done.1, f32[1024,512,8]{1,0,2:T(8,128)S(1)} %get-tuple-element.334, f32[8,512]{1,0:T(8,128)S(1)} %get-tuple-element.332, pred[512,1024]{0,1:T(8,128)(4,1)S(1)} %compare_and_fusion.2, f32[8,512]{1,0:T(8,128)S(1)} %get-tuple-element.336, ...), kind=kOutput, calls=%fused_computation.11.clone.1 | convolution fusion | flops 1096810496 | bytes 21807108 | tf_op jit(solution)/shard_map/while/body/eval_jaxpr/kgrc,ckd->kgrd/dot_general | solution.py:35
  141.1 0.0 copy-start.2
  141.2 1.3 copy-done.2
  142.5 2.0 %fusion.26 = bf16[512,1,8,128]{3,0,2,1:T(8,128)(2,1)S(1)} fusion(f32[1,8,512,128]{3,2,1,0:T(8,128)} %get-tuple-element.175, f32[8,512]{1,0:T(8,128)S(1)} %bitcast.122), kind=kLoop, calls=%fused_computation.42 | loop fusion | flops 1048576 | bytes 3162112 | tf_op jit(solution)/shard_map/convert_element_type | solution.py:105
  144.4 0.7 copy.19
  145.1 0.5 convert_element_type.19
  145.6 30.0 %all_to_all.70 = bf16[8,64,1024]{2,1,0:T(8,128)(2,1)S(1)} all-to-all(bf16[8,64,1024]{2,1,0:T(8,128)(2,1)S(1)} %convert_element_type.19), channel_id=1, replica_groups=mesh['head'=8,'kv'=4] {'head'}, dimensions={0} | all-to-all | bytes 2097152 | tf_op jit(solution)/shard_map/all_to_all | solution.py:106
  175.6 1.1 copy.25
  (21 shorter events, 0.2 us)
Async XLA Ops:
  0.0 0.9 copy-start
  1.6 13.1 %all-to-all-start = ((bf16[64,8,128]{2,0,1:T(8,128)(2,1)}), bf16[64,8,128]{2,0,1:T(8,128)(2,1)S(1)}, u32[]{:S(2)}, u32[]{:S(2)}) async-start(bf16[64,8,128]{2,0,1:T(8,128)(2,1)} %copy_bitcast_fusion.2), calls=%async_computation | async-start | bytes 262144 | tf_op jit(solution)/shard_map/all_to_all | solution.py:66
  14.7 10.1 %all-to-all-start.2 = ((bf16[64,8,128]{2,0,1:T(8,128)(2,1)}), bf16[64,8,128]{2,0,1:T(8,128)(2,1)S(1)}, u32[]{:S(2)}, u32[]{:S(2)}) async-start(bf16[64,8,128]{2,0,1:T(8,128)(2,1)} %copy_bitcast_fusion.1), calls=%async_computation.2 | async-start | bytes 262144 | tf_op jit(solution)/shard_map/all_to_all | solution.py:67
  24.8 74.1 %all-to-all-start.1 = ((bf16[64,8,1024]{2,0,1:T(8,128)(2,1)}), bf16[64,8,1024]{2,0,1:T(8,128)(2,1)S(1)}, u32[]{:S(2)}, u32[]{:S(2)}) async-start(bf16[64,8,1024]{2,0,1:T(8,128)(2,1)} %bitcast.93), calls=%async_computation.1 | async-start | bytes 2097152 | tf_op jit(solution)/shard_map/all_to_all | solution.py:65
  109.3 4.1 %copy-start.1 = (f32[1,8,512,128]{3,2,1,0:T(8,128)S(1)}, f32[1,8,512,128]{3,2,1,0:T(8,128)}, u32[]{:S(2)}) copy-start(f32[1,8,512,128]{3,2,1,0:T(8,128)} %get-tuple-element.355) | copy-start | bytes 6291460 | tf_op jit(solution)/shard_map/while
  119.6 1.3 copy-start.2
  130.9 4.1 %copy-start.1 = (f32[1,8,512,128]{3,2,1,0:T(8,128)S(1)}, f32[1,8,512,128]{3,2,1,0:T(8,128)}, u32[]{:S(2)}) copy-start(f32[1,8,512,128]{3,2,1,0:T(8,128)} %get-tuple-element.355) | copy-start | bytes 6291460 | tf_op jit(solution)/shard_map/while
  141.1 1.3 copy-start.2
where the time goes:
time: 177 us
  blocking collectives  94.4 us (53%)
  local copies, waits for them, and re-layouts  28.4 us (16%)
  matrix products  18.1 us (10%)
  starting transfers between devices  13.3 us (8%)
  other arithmetic  11.8 us (7%)
  waiting for transfers between devices  9.58 us (5%)
    unnamed x1, blocking collectives  43.9 us
    all_to_all x1, blocking collectives, local(): lax.all_to_all(result, 'head', split_axis=0, concat_axis=1, tiled=True)  30 us
    gather x2, local copies, waits for them, and re-layouts, one_step(): key_doc = jnp.take(doc_global, key_pos)  12.3 us
    dot_general x2, matrix products, block_terms(): jnp.einsum('kgrc,ckd->kgrd', weights.astype(jnp.bfloat16), value_heads, p...  12.3 us
    all_gather x1, blocking collectives, local(): value_piece = lax.all_gather(value_block, 'kv', axis=0, tiled=True)  11.6 us
    all_gather x1, blocking collectives, local(): key_piece = lax.all_gather(key_block, 'kv', axis=0, tiled=True)  9 us
    reduce_sum x2, other arithmetic, block_terms(): row_total = jnp.sum(weights, axis=-1)  8.05 us
    all_to_all x1, starting transfers between devices, local(): lax.all_to_all(key_send, 'head', split_axis=1, concat_axis=0, tiled=True)  6.35 us
  transfers between devices with their start and end apart: 3, of which 2 were waited for; matrix products, arithmetic and copies ran while one was open for 5% of the time, Pallas kernels for 0%

commit v1 on v0

--- a/solution.py
+++ b/solution.py
@@ -83,7 +83,13 @@
         jnp.zeros(term_shape + (HEAD_SIZE,), jnp.float32),
     )
     key_piece = lax.all_gather(key_block, "kv", axis=0, tiled=True)
-    value_piece = lax.all_gather(value_block, "kv", axis=0, tiled=True)
+    count = lax.axis_size("kv")
+    moving, parts = (value_block, [value_block])
+    for _ in range(count - 1):
+        moving = lax.ppermute(moving, "kv", [(i, (i + 1) % count) for i in range(count)])
+        parts.insert(0, moving)
+    flat = jnp.concatenate(parts, axis=0)
+    value_piece = jnp.roll(flat, (lax.axis_index("kv") + 1) * value_block.shape[0], axis=0)
     piece_rows = key_piece.shape[0]
     step_rows = math.gcd(piece_rows, 1024)
 

time: 177 us -> 170 us (0.960)
  blocking collectives: 94.4 us -> 83 us
  starting transfers between devices: 13.3 us -> 18.7 us
    all_gather x1 -> x0, blocking collectives: 11.6 us -> none  [local(): value_piece = lax.all_gather(value_block, 'kv', axis=0, tiled=True)]
    ppermute x0 -> x3, starting transfers between devices: none -> 5.41 us  [local(): lax.ppermute(moving, 'kv', [(i, (i + 1) % count) for i in range(count)])]
    all_to_all x1, starting transfers between devices: 6.35 us -> 3.37 us  [local(): lax.all_to_all(key_send, 'head', split_axis=1, concat_axis=0, tiled=True)]
    all_to_all x1, starting transfers between devices: 3.37 us -> 6.35 us  [local(): lax.all_to_all(value_send, 'head', split_axis=1, concat_axis=0, tiled=True)]
    all_to_all x1, waiting for transfers between devices: 5.18 us -> 2.86 us  [local(): lax.all_to_all(key_send, 'head', split_axis=1, concat_axis=0, tiled=True)]
    unnamed x7 -> x14, local copies, waits for them, and re-layouts: 3.49 us -> 3.62 us
  transfers between devices with their start and end apart: 3 -> 6, of which waited for: 2 -> 2; matrix products, arithmetic and copies ran while one was open for 5% -> 6% of each run, Pallas kernels for 0% -> 0%
where the time goes in v1:
time: 170 us
  blocking collectives  83 us (49%)
  local copies, waits for them, and re-layouts  28.6 us (17%)
  starting transfers between devices  18.7 us (11%)
  matrix products  18.3 us (11%)
  other arithmetic  11.8 us (7%)
  waiting for transfers between devices  8.04 us (5%)
    unnamed x1, blocking collectives  42.4 us
    all_to_all x1, blocking collectives, local(): lax.all_to_all(result, 'head', split_axis=0, concat_axis=1, tiled=True)  30 us
    dot_general x2, matrix products, block_terms(): jnp.einsum('kgrc,ckd->kgrd', weights.astype(jnp.bfloat16), value_heads, p...  12.5 us
    gather x2, local copies, waits for them, and re-layouts, one_step(): key_doc = jnp.take(doc_global, key_pos)  12.3 us
    all_gather x1, blocking collectives, local(): key_piece = lax.all_gather(key_block, 'kv', axis=0, tiled=True)  10.7 us
    reduce_sum x2, other arithmetic, block_terms(): row_total = jnp.sum(weights, axis=-1)  8.05 us
    all_to_all x1, starting transfers between devices, local(): lax.all_to_all(value_send, 'head', split_axis=1, concat_axis=0, tiled=True)  6.35 us
    dot_general x2, matrix products, block_terms(): jnp.einsum('rkgd,ckd->kgrc', query_group, key_heads, preferred_element_ty...  5.86 us
  transfers between devices with their start and end apart: 6, of which 2 were waited for; matrix products, arithmetic and copies ran while one was open for 6% of the time, Pallas kernels for 0%

profile of v1, /device:TPU:0, one launch (start us, length us, event | category | flops | bytes accessed | tf_op | source)
XLA Modules:
  0.0 169.8 jit_solution(5055893882364015732)
XLA Ops:
  0.0 0.0 copy-start
  0.0 0.9 copy-done
  0.9 0.7 copy_bitcast_fusion.1
  1.6 6.4 %all-to-all-start.2 = ((bf16[64,8,128]{2,0,1:T(8,128)(2,1)}), bf16[64,8,128]{2,0,1:T(8,128)(2,1)S(1)}, u32[]{:S(2)}, u32[]{:S(2)}) async-start(bf16[64,8,128]{2,0,1:T(8,128)(2,1)} %copy_bitcast_fusion.1), calls=%async_computation.2 | async-start | bytes 262144 | tf_op jit(solution)/shard_map/all_to_all | solution.py:67
  7.9 1.6 copy_bitcast_fusion.2
  9.5 5.2 %all-to-all-done.2 = bf16[64,8,128]{2,0,1:T(8,128)(2,1)S(1)} async-done(((bf16[64,8,128]{2,0,1:T(8,128)(2,1)}), bf16[64,8,128]{2,0,1:T(8,128)(2,1)S(1)}, u32[]{:S(2)}, u32[]{:S(2)}) %all-to-all-start.2) | async-done | bytes 131104 | tf_op jit(solution)/shard_map/all_to_all | solution.py:67
  14.7 3.4 %all-to-all-start = ((bf16[64,8,128]{2,0,1:T(8,128)(2,1)}), bf16[64,8,128]{2,0,1:T(8,128)(2,1)S(1)}, u32[]{:S(2)}, u32[]{:S(2)}) async-start(bf16[64,8,128]{2,0,1:T(8,128)(2,1)} %copy_bitcast_fusion.2), calls=%async_computation | async-start | bytes 262144 | tf_op jit(solution)/shard_map/all_to_all | solution.py:66
  18.1 1.5 collective-permute-start
  19.6 2.3 %copy.30 = bf16[8,8,8,1024]{3,2,0,1:T(8,128)(2,1)} copy(bf16[8,8,8,1024]{3,2,1,0:T(8,128)(2,1)} %bitcast.124) | data formatting | bytes 2097152 | tf_op jit(solution)/shard_map/all_to_all | solution.py:65
  21.9 2.9 %all-to-all-done = bf16[64,8,128]{2,0,1:T(8,128)(2,1)S(1)} async-done(((bf16[64,8,128]{2,0,1:T(8,128)(2,1)}), bf16[64,8,128]{2,0,1:T(8,128)(2,1)S(1)}, u32[]{:S(2)}, u32[]{:S(2)}) %all-to-all-start) | async-done | bytes 131104 | tf_op jit(solution)/shard_map/all_to_all | solution.py:66
  24.8 3.6 %all-to-all-start.1 = ((bf16[64,8,1024]{2,0,1:T(8,128)(2,1)}), bf16[64,8,1024]{2,0,1:T(8,128)(2,1)S(1)}, u32[]{:S(2)}, u32[]{:S(2)}) async-start(bf16[64,8,1024]{2,0,1:T(8,128)(2,1)} %bitcast.93), calls=%async_computation.1 | async-start | bytes 2097152 | tf_op jit(solution)/shard_map/all_to_all | solution.py:65
  28.3 0.0 collective-permute-done
  28.3 1.5 collective-permute-start.1
  29.9 1.3 dynamic-slice
  31.9 0.9 dynamic-update-slice
  32.8 42.4 %all-reduce = s32[2048]{0:T(1024)S(1)} all-reduce(s32[2048]{0:T(1024)S(1)} %dynamic-update-slice), channel_id=1, replica_groups=mesh['head'=8,'kv'=4] {'kv','head'}, use_global_device_ids=true, to_apply=%add | all-reduce | flops 2048 | bytes 16384
  75.1 3.1 %gather_fusion.1 = s32[512]{0:T(512)S(1)} fusion(s32[2048]{0:T(1024)S(1)} %all-reduce, s32[1024]{0:T(1024)S(1)} %pad_clamp_fusion), kind=kCustom, calls=%fused_computation.1 | custom fusion | bytes 6144 | tf_op jit(solution)/shard_map/jit(_take)/gather | solution.py:77
  78.3 0.0 collective-permute-done.1
  78.3 2.3 %collective-permute-start.2 = (bf16[512,128]{1,0:T(8,128)(2,1)S(1)}, bf16[512,128]{1,0:T(8,128)(2,1)S(1)}, u32[]{:S(2)}, u32[]{:S(2)}) collective-permute-start(bf16[512,128]{1,0:T(8,128)(2,1)S(1)} %collective-permute-done.1), channel_id=1, source_target_pairs={{0,1},{1,2},{2,3},{3,0},{4,5},{5,6},{6,7},{7,4},{8,9},{9,10},{10,1... | collective-permute-start | bytes 393224 | tf_op jit(solution)/shard_map/ppermute | solution.py:89
  80.6 10.7 %all_gather.7 = bf16[2048,128]{1,0:T(8,128)(2,1)S(1)} all-gather(bf16[512,128]{1,0:T(8,128)(2,1)S(1)} %bitcast.126), channel_id=1, replica_groups=mesh['head'=8,'kv'=4] {'kv'}, dimensions={0}, use_global_device_ids=true | all-gather | bytes 655360 | tf_op jit(solution)/shard_map/all_gather | solution.py:85
  91.3 0.0 collective-permute-done.2
  91.6 0.0 all-to-all-done.1
  91.6 0.3 copy.26
  91.9 0.1 copy.18
  92.0 43.6 %while.18 = (s32[]{:T(128)}, f32[1,8,512]{2,1,0:T(8,128)S(1)}, f32[1,8,512]{2,1,0:T(8,128)S(1)}, f32[1,8,512,128]{3,2,1,0:T(8,128)}, s32[2048]{0:T(1024)S(1)}, /...) while((s32[]{:T(128)}, f32[1,8,512]{2,1,0:T(8,128)S(1)}, ...), condition=%wide.region_3.4_spmd.clone, body=%wide.region_0.3_spmd.clone.sunk | while | flops 2205726208 | bytes 75335952 | solution.py:107
  92.3 6.2 %gather_fusion = s32[1024]{0:T(1024)S(1)} fusion(s32[2048]{0:T(1024)S(1)} %get-tuple-element.370, s32[1024]{0:T(1024)S(1)} %broadcast_clamp_fusion.2), kind=kCustom, calls=%fused_computation.clone.clone.1 | custom fusion | bytes 12288 | tf_op jit(solution)/shard_map/while/body/eval_jaxpr/jit(_take)/gather | solution.py:101
  98.5 0.8 compare_and_fusion.2
  99.3 2.9 %fusion.41 = (f32[8,512]{1,0:T(8,128)S(1)}, f32[1024,512,8]{1,0,2:T(8,128)S(1)}) fusion(pred[512,1024]{0,1:T(8,128)(4,1)S(1)} %compare_and_fusion.2, bf16[512,1,8,128]{3,0,2,1:T(8,128)(2,1)S(1)} %get-tuple-element.373, bf16[2048,128]{1,0:T(8,128)(2,1)S(1)} %get-tuple-element.372, s32[]{:T(128)S(6)} %select_n.160), kind=kOutput, calls=%fused_computation.5.clone.1 | convolution fusion | flops 1086320640 | bytes 18628612 | tf_op jit(solution)/shard_map/while/body/eval_jaxpr/rkgd,ckd->kgrc/dot_general | solution.py:27
  102.2 0.0 copy-start.1
  102.3 4.0 %fusion.43 = f32[8,512]{1,0:T(8,128)S(1)} fusion(f32[1024,512,8]{1,0,2:T(8,128)S(1)} %get-tuple-element.334, f32[8,512]{1,0:T(8,128)S(1)} %get-tuple-element.332, pred[512,1024]{0,1:T(8,128)(4,1)S(1)} %compare_and_fusion.2), kind=kLoop, calls=%fused_computation.7.clone.1 | loop fusion | flops 20967424 | bytes 17334272 | tf_op jit(solution)/shard_map/while/body/eval_jaxpr/reduce_sum | solution.py:34
  106.3 0.0 copy-done.1
  106.4 6.2 %bitcast_add_fusion.2 = f32[1,8,512,128]{3,2,1,0:T(8,128)S(1)} fusion(f32[1,8,512,128]{3,2,1,0:T(8,128)S(1)} %copy-done.1, f32[1024,512,8]{1,0,2:T(8,128)S(1)} %get-tuple-element.334, f32[8,512]{1,0:T(8,128)S(1)} %get-tuple-element.332, pred[512,1024]{0,1:T(8,128)(4,1)S(1)} %compare_and_fusion.2, f32[8,512]{1,0:T(8,128)S(1)} %get-tuple-element.336, ...), kind=kOutput, calls=%fused_computation.11.clone.1 | convolution fusion | flops 1096810496 | bytes 21807108 | tf_op jit(solution)/shard_map/while/body/eval_jaxpr/kgrc,ckd->kgrd/dot_general | solution.py:35
  112.6 0.0 copy-start.2
  112.6 1.3 copy-done.2
  114.0 6.2 %gather_fusion = s32[1024]{0:T(1024)S(1)} fusion(s32[2048]{0:T(1024)S(1)} %get-tuple-element.370, s32[1024]{0:T(1024)S(1)} %broadcast_clamp_fusion.2), kind=kCustom, calls=%fused_computation.clone.clone.1 | custom fusion | bytes 12288 | tf_op jit(solution)/shard_map/while/body/eval_jaxpr/jit(_take)/gather | solution.py:101
  120.2 0.8 compare_and_fusion.2
  121.0 2.9 %fusion.41 = (f32[8,512]{1,0:T(8,128)S(1)}, f32[1024,512,8]{1,0,2:T(8,128)S(1)}) fusion(pred[512,1024]{0,1:T(8,128)(4,1)S(1)} %compare_and_fusion.2, bf16[512,1,8,128]{3,0,2,1:T(8,128)(2,1)S(1)} %get-tuple-element.373, bf16[2048,128]{1,0:T(8,128)(2,1)S(1)} %get-tuple-element.372, s32[]{:T(128)S(6)} %select_n.160), kind=kOutput, calls=%fused_computation.5.clone.1 | convolution fusion | flops 1086320640 | bytes 18628612 | tf_op jit(solution)/shard_map/while/body/eval_jaxpr/rkgd,ckd->kgrc/dot_general | solution.py:27
  124.0 0.0 copy-start.1
  124.0 4.0 %fusion.43 = f32[8,512]{1,0:T(8,128)S(1)} fusion(f32[1024,512,8]{1,0,2:T(8,128)S(1)} %get-tuple-element.334, f32[8,512]{1,0:T(8,128)S(1)} %get-tuple-element.332, pred[512,1024]{0,1:T(8,128)(4,1)S(1)} %compare_and_fusion.2), kind=kLoop, calls=%fused_computation.7.clone.1 | loop fusion | flops 20967424 | bytes 17334272 | tf_op jit(solution)/shard_map/while/body/eval_jaxpr/reduce_sum | solution.py:34
  128.1 0.0 copy-done.1
  128.1 6.2 %bitcast_add_fusion.2 = f32[1,8,512,128]{3,2,1,0:T(8,128)S(1)} fusion(f32[1,8,512,128]{3,2,1,0:T(8,128)S(1)} %copy-done.1, f32[1024,512,8]{1,0,2:T(8,128)S(1)} %get-tuple-element.334, f32[8,512]{1,0:T(8,128)S(1)} %get-tuple-element.332, pred[512,1024]{0,1:T(8,128)(4,1)S(1)} %compare_and_fusion.2, f32[8,512]{1,0:T(8,128)S(1)} %get-tuple-element.336, ...), kind=kOutput, calls=%fused_computation.11.clone.1 | convolution fusion | flops 1096810496 | bytes 21807108 | tf_op jit(solution)/shard_map/while/body/eval_jaxpr/kgrc,ckd->kgrd/dot_general | solution.py:35
  134.3 0.0 copy-start.2
  134.3 1.3 copy-done.2
  135.7 2.0 %fusion.26 = bf16[512,1,8,128]{3,0,2,1:T(8,128)(2,1)S(1)} fusion(f32[1,8,512,128]{3,2,1,0:T(8,128)} %get-tuple-element.175, f32[8,512]{1,0:T(8,128)S(1)} %bitcast.125), kind=kLoop, calls=%fused_computation.42 | loop fusion | flops 1048576 | bytes 3162112 | tf_op jit(solution)/shard_map/convert_element_type | solution.py:111
  137.6 0.7 copy.19
  138.3 0.5 convert_element_type.19
  138.8 30.0 %all_to_all.70 = bf16[8,64,1024]{2,1,0:T(8,128)(2,1)S(1)} all-to-all(bf16[8,64,1024]{2,1,0:T(8,128)(2,1)S(1)} %convert_element_type.19), channel_id=1, replica_groups=mesh['head'=8,'kv'=4] {'head'}, dimensions={0} | all-to-all | bytes 2097152 | tf_op jit(solution)/shard_map/all_to_all | solution.py:112
  168.8 1.1 copy.25
  (30 shorter events, 0.3 us)
Async XLA Ops:
  0.0 0.9 copy-start
  1.6 13.1 %all-to-all-start.2 = ((bf16[64,8,128]{2,0,1:T(8,128)(2,1)}), bf16[64,8,128]{2,0,1:T(8,128)(2,1)S(1)}, u32[]{:S(2)}, u32[]{:S(2)}) async-start(bf16[64,8,128]{2,0,1:T(8,128)(2,1)} %copy_bitcast_fusion.1), calls=%async_computation.2 | async-start | bytes 262144 | tf_op jit(solution)/shard_map/all_to_all | solution.py:67
  14.7 10.1 %all-to-all-start = ((bf16[64,8,128]{2,0,1:T(8,128)(2,1)}), bf16[64,8,128]{2,0,1:T(8,128)(2,1)S(1)}, u32[]{:S(2)}, u32[]{:S(2)}) async-start(bf16[64,8,128]{2,0,1:T(8,128)(2,1)} %copy_bitcast_fusion.2), calls=%async_computation | async-start | bytes 262144 | tf_op jit(solution)/shard_map/all_to_all | solution.py:66
  18.1 10.3 %collective-permute-start = (bf16[512,128]{1,0:T(8,128)(2,1)S(1)}, bf16[512,128]{1,0:T(8,128)(2,1)S(1)}, u32[]{:S(2)}, u32[]{:S(2)}) collective-permute-start(bf16[512,128]{1,0:T(8,128)(2,1)S(1)} %bitcast.121), channel_id=1, source_target_pairs={{0,1},{1,2},{2,3},{3,0},{4,5},{5,6},{6,7},{7,4},{8,9},{9,10},{10,1... | collective-permute-start | bytes 393224 | tf_op jit(solution)/shard_map/ppermute | solution.py:89
  24.8 66.9 %all-to-all-start.1 = ((bf16[64,8,1024]{2,0,1:T(8,128)(2,1)}), bf16[64,8,1024]{2,0,1:T(8,128)(2,1)S(1)}, u32[]{:S(2)}, u32[]{:S(2)}) async-start(bf16[64,8,1024]{2,0,1:T(8,128)(2,1)} %bitcast.93), calls=%async_computation.1 | async-start | bytes 2097152 | tf_op jit(solution)/shard_map/all_to_all | solution.py:65
  28.3 49.9 %collective-permute-start.1 = (bf16[512,128]{1,0:T(8,128)(2,1)S(1)}, bf16[512,128]{1,0:T(8,128)(2,1)S(1)}, u32[]{:S(2)}, u32[]{:S(2)}) collective-permute-start(bf16[512,128]{1,0:T(8,128)(2,1)S(1)} %collective-permute-done), channel_id=1, source_target_pairs={{0,1},{1,2},{2,3},{3,0},{4,5},{5,6},{6,7},{7,4},{8,9},{9,10},{10,1... | collective-permute-start | bytes 393224 | tf_op jit(solution)/shard_map/ppermute | solution.py:89
  78.3 13.1 %collective-permute-start.2 = (bf16[512,128]{1,0:T(8,128)(2,1)S(1)}, bf16[512,128]{1,0:T(8,128)(2,1)S(1)}, u32[]{:S(2)}, u32[]{:S(2)}) collective-permute-start(bf16[512,128]{1,0:T(8,128)(2,1)S(1)} %collective-permute-done.1), channel_id=1, source_target_pairs={{0,1},{1,2},{2,3},{3,0},{4,5},{5,6},{6,7},{7,4},{8,9},{9,10},{10,1... | collective-permute-start | bytes 393224 | tf_op jit(solution)/shard_map/ppermute | solution.py:89
  102.2 4.1 %copy-start.1 = (f32[1,8,512,128]{3,2,1,0:T(8,128)S(1)}, f32[1,8,512,128]{3,2,1,0:T(8,128)}, u32[]{:S(2)}) copy-start(f32[1,8,512,128]{3,2,1,0:T(8,128)} %get-tuple-element.355) | copy-start | bytes 6291460 | tf_op jit(solution)/shard_map/while
  112.6 1.3 copy-start.2
  124.0 4.1 %copy-start.1 = (f32[1,8,512,128]{3,2,1,0:T(8,128)S(1)}, f32[1,8,512,128]{3,2,1,0:T(8,128)}, u32[]{:S(2)}) copy-start(f32[1,8,512,128]{3,2,1,0:T(8,128)} %get-tuple-element.355) | copy-start | bytes 6291460 | tf_op jit(solution)/shard_map/while
  134.3 1.3 copy-start.2
